TPU v7x, 32 devices: a whole 2x2x4 slice. The times are simulated.
32 devices in a mesh: dp: 4 (over z), expert: 2 (over y), mp: 4 (over x, core).
Axes of the slice: x: 2, y: 2, z: 4, core: 2. Of those that a mesh axis runs over, the one named last changes fastest.
Arguments:
- tokens: bfloat16 [1024, 2048], P(('dp', 'expert'), 'mp'), may hold values from -6 to 6
- targets: bfloat16 [1024, 2048], P(('dp', 'expert'), 'mp'), may hold values from -6 to 6
- token_weight: float32 [1024], P(('dp', 'expert')), may hold values from 0.5 to 11.7, as said below
- routes: int32 [1024, 2], P(('dp', 'expert')), may hold values from 0 to 7, all different within a row; in each aligned block of 128 rows (0 to 127, 128 to 255, ...) at most 40 rows name the same one
- router_weight: bfloat16 [2048, 8], P('mp'), may hold values from -0.125 to 0.125
- base_weight: bfloat16 [3, 8, 2048, 8192], P(None, 'expert', None, ('dp', 'mp')), may hold values from -0.125 to 0.125
- direction_one: bfloat16 [3, 8, 2048, 8192], P(None, 'expert', None, ('dp', 'mp')), may hold values from -0.125 to 0.125
- direction_two: bfloat16 [3, 8, 2048, 8192], P(None, 'expert', None, ('dp', 'mp')), may hold values from -0.125 to 0.125
- filter_scale: float32 [2, 8, 8192], P(None, 'expert', ('dp', 'mp')), may hold values from 0.5 to 2
- landscape: float32 [2], replicated, may hold values from -0.6 to 0.6
Outputs:
- mixed: bfloat16 [1024, 2048], P(('dp', 'expert'), 'mp')
- loss: float32 [1], replicated
Inputs may be any that keep to these rules, and one draw needn't show every extreme that they name: `routes`: each row names 2 different experts. Within the rows of one group of dp and expert (aligned blocks of 128 rows) no expert is named more than 40 times, a bound that some block reaches. `token_weight`: Positive.
All inputs are finite; a program needn't handle non-finite values.
Results may differ from a plain program's by a relative error of at most 0.0028.
The roundings to bfloat16 on the way count: a program that leaves them out, or rounds other values in their place, can miss the bound.
Values may be sent and summed in bfloat16 or wider, within the bound.
A program may use at most 192 MiB of HBM per device.

v0:
```python
import jax
import jax.numpy as jnp
from jax import lax
from jax.sharding import PartitionSpec as P

CAP = 40


def rebuild(base_weight, direction_one, direction_two, filter_scale, landscape):
    scale_one = filter_scale[0][None, :, None, :]
    scale_two = filter_scale[1][None, :, None, :]
    merged = (
        base_weight.astype(jnp.float32)
        + landscape[0] * scale_one * direction_one.astype(jnp.float32)
        + landscape[1] * scale_two * direction_two.astype(jnp.float32)
    )
    return merged.astype(jnp.bfloat16)


def slot_target(routes, expert_count, capacity):
    pair_ids = jnp.concatenate([routes[:, 0], routes[:, 1]])
    expert_ids = jnp.arange(expert_count, dtype=jnp.int32)
    onehot = (pair_ids[:, None] == expert_ids[None, :]).astype(jnp.int32)
    earlier = jnp.cumsum(onehot, axis=0) - onehot
    slot = jnp.sum(earlier * onehot, axis=1)
    return pair_ids * capacity + slot


def per_device(
    tokens,
    targets,
    token_weight,
    routes,
    router_weight,
    base_weight,
    direction_one,
    direction_two,
    filter_scale,
    landscape,
):
    tok_rows, feat_local = tokens.shape
    expert_count = router_weight.shape[1]
    local_experts = base_weight.shape[1]
    model_width = base_weight.shape[2]
    hidden_local = base_weight.shape[3]
    expert_devices = lax.axis_size("expert")
    dp_count = lax.axis_size("dp")
    mp_count = lax.axis_size("mp")
    partial_logits = jnp.dot(tokens, router_weight, preferred_element_type=jnp.float32)
    logits = lax.psum(partial_logits, "mp")
    expert_ids = jnp.arange(expert_count, dtype=jnp.int32)
    pick_first = jnp.sum(jnp.where(routes[:, 0:1] == expert_ids[None, :], logits, 0.0), axis=1)
    pick_second = jnp.sum(jnp.where(routes[:, 1:2] == expert_ids[None, :], logits, 0.0), axis=1)
    gate_first = 1.0 / (1.0 + jnp.exp(pick_second - pick_first))
    gate_second = 1.0 / (1.0 + jnp.exp(pick_first - pick_second))
    flat_index = slot_target(routes, expert_count, CAP)
    placer = (
        flat_index[:, None] == jnp.arange(expert_count * CAP, dtype=jnp.int32)[None, :]
    ).astype(jnp.bfloat16)
    source = lax.all_gather(tokens, "mp", axis=1, tiled=True)
    doubled = jnp.concatenate([source, source], axis=0)
    buffer = jnp.einsum("pk,pf->kf", placer, doubled, preferred_element_type=jnp.float32).astype(
        jnp.bfloat16
    )
    buffer = buffer.reshape(expert_count, CAP, source.shape[1])
    received = lax.all_to_all(buffer, "expert", split_axis=0, concat_axis=0, tiled=True)
    slots = received.reshape(expert_devices, local_experts, CAP, model_width)
    rebuilt = rebuild(base_weight, direction_one, direction_two, filter_scale, landscape)
    shard_piece = lax.all_gather(slots, "dp", axis=0, tiled=True)
    gate_value = jnp.einsum(
        "njqd,jdh->njqh", shard_piece, rebuilt[0], preferred_element_type=jnp.float32
    )
    up_value = jnp.einsum(
        "njqd,jdh->njqh", shard_piece, rebuilt[1], preferred_element_type=jnp.float32
    )
    hidden = (jax.nn.silu(gate_value) * up_value).astype(jnp.bfloat16)
    hidden_groups = hidden.reshape(dp_count, expert_devices, local_experts, CAP, hidden_local)
    down_blocks = (
        rebuilt[2].reshape(local_experts, mp_count, feat_local, hidden_local).transpose(1, 0, 2, 3)
    )
    positions = jnp.arange(1 * lax.axis_size(("dp", "mp")), dtype=jnp.int32)
    chosen_rows = jnp.take(hidden_groups, positions // mp_count, axis=0)
    chosen_cols = jnp.take(down_blocks, positions % mp_count, axis=0)
    summed = lax.psum_scatter(
        jnp.einsum(
            "cnjqh,cjfh->cnjqf", chosen_rows, chosen_cols, preferred_element_type=jnp.float32
        ),
        ("dp", "mp"),
        scatter_dimension=0,
        tiled=True,
    )
    expert_out = summed[0].astype(jnp.bfloat16)
    returned = lax.all_to_all(expert_out, "expert", split_axis=0, concat_axis=0, tiled=True)
    out_rows = returned.reshape(expert_count * CAP, feat_local)
    first_out = jnp.take(out_rows, flat_index[:tok_rows], axis=0).astype(jnp.float32)
    second_out = jnp.take(out_rows, flat_index[tok_rows:], axis=0).astype(jnp.float32)
    combined = (
        tokens.astype(jnp.float32)
        + gate_first[:, None] * first_out
        + gate_second[:, None] * second_out
    )
    error = combined - targets.astype(jnp.float32)
    partial_loss = jnp.sum(token_weight[:, None] * error * error)
    loss_total = lax.psum(partial_loss, ("dp", "expert", "mp"))
    entries = tok_rows * dp_count * expert_devices * feat_local * mp_count
    loss = (loss_total / entries).reshape(1)
    return (combined.astype(jnp.bfloat16), loss)


def solution(mesh):
    in_specs = (
        P(("dp", "expert"), "mp"),
        P(("dp", "expert"), "mp"),
        P(("dp", "expert")),
        P(("dp", "expert"), None),
        P("mp", None),
        P(None, "expert", None, ("dp", "mp")),
        P(None, "expert", None, ("dp", "mp")),
        P(None, "expert", None, ("dp", "mp")),
        P(None, "expert", ("dp", "mp")),
        P(),
    )
    out_specs = (P(("dp", "expert"), "mp"), P())
    return jax.shard_map(
        per_device, mesh=mesh, in_specs=in_specs, out_specs=out_specs, check_vma=False
    )
```

profile of v0, /device:TPU:0, one launch (start us, length us, event | category | flops | bytes accessed | tf_op | source)
XLA Modules:
  0.0 359.5 jit_solution(4609042770044115656)
XLA Ops:
  9.0 8.9 %all_gather.6 = bf16[128,2048]{1,0:T(8,128)(2,1)S(1)} all-gather(bf16[128,512]{1,0:T(8,128)(2,1)} %param.12), channel_id=1, replica_groups=mesh['dp'=4,'expert'=2,'mp'=4] {'mp'}, dimensions={1}, use_global_device_ids=true | all-gather | bytes 655360 | tf_op jit(solution)/shard_map/all_gather | solution.py:60
  18.5 19.7 %all_to_all.10 = bf16[8,40,2048]{2,1,0:T(8,128)(2,1)S(1)} all-to-all(bf16[8,40,2048]{2,1,0:T(8,128)(2,1)S(1)} %bitcast.83), channel_id=1, replica_groups=mesh['dp'=4,'expert'=2,'mp'=4] {'expert'}, dimensions={0} | all-to-all | bytes 2621440 | tf_op jit(solution)/shard_map/all_to_all | solution.py:66
  38.1 1.2 copy.14
  40.1 1.3 multiply_bitcast_fusion.1
  41.4 34.5 %add_convert_fusion = bf16[3,4,2048,512]{3,2,1,0:T(8,128)(2,1)} fusion(bf16[3,4,2048,512]{3,2,1,0:T(8,128)(2,1)} %param.19, bf16[3,4,2048,512]{3,2,1,0:T(8,128)(2,1)} %param.18, bf16[3,4,2048,512]{3,2,1,0:T(8,128)(2,1)} %param.17, f32[4,512]{1,0:T(4,128)S(1)} %get-tuple-element.14, f32[4,512]{1,0:T(4,128)S(1)} %get-tuple-element.13), kind=kLoop, calls=%fused_computation.5 | loop fusion | flops 100663296 | bytes 100679680 | tf_op jit(solution)/shard_map/convert_element_type | solution.py:17
  75.9 7.2 %slice.65 = bf16[1,4,2048,512]{3,2,1,0:T(8,128)(2,1)} slice(bf16[3,4,2048,512]{3,2,1,0:T(8,128)(2,1)} %add_convert_fusion), slice={[2:3], [0:4], [0:2048], [0:512]} | slice | bytes 16777216 | tf_op jit(solution)/shard_map/slice | solution.py:79
  83.1 5.9 %fusion.34 = (bf16[4,4,256,512]{3,2,0,1:T(8,128)(2,1)}, bf16[4,4,256,512]{3,2,0,1:T(8,128)(2,1)}) fusion(bf16[4,4,512,512]{3,2,0,1:T(8,128)(2,1)} %bitcast.78), kind=kLoop, calls=%fused_computation.88 | loop fusion | bytes 16777216 | tf_op jit(solution)/shard_map/jit(_take)/gather | solution.py:83
  89.0 9.2 %gather_fusion.1 = bf16[16,4,256,512]{3,2,1,0:T(8,128)(2,1)} fusion(bf16[4,4,256,512]{3,2,0,1:T(8,128)(2,1)} %get-tuple-element.9, s32[1024]{0:T(1024)S(1)} %pad_clamp_fusion.3), kind=kCustom, calls=%fused_computation.3 | custom fusion | bytes 33554496 | tf_op jit(solution)/shard_map/jit(_take)/gather | solution.py:83
  98.1 9.1 %gather_fusion.2 = bf16[16,4,256,512]{3,2,1,0:T(8,128)(2,1)} fusion(bf16[4,4,256,512]{3,2,0,1:T(8,128)(2,1)} %get-tuple-element.10, s32[1024]{0:T(1024)S(1)} %pad_clamp_fusion.3), kind=kCustom, calls=%fused_computation.4 | custom fusion | bytes 33554496 | tf_op jit(solution)/shard_map/jit(_take)/gather | solution.py:83
  107.3 30.2 %all-gather.2.cloned.1.call-done = bf16[8,4,40,2048]{3,2,0,1:T(8,128)(2,1)} async-done(((bf16[2,4,40,2048]{3,2,0,1:T(8,128)(2,1)}), bf16[8,4,40,2048]{3,2,0,1:T(8,128)(2,1)}) %all-gather.2.cloned.1.call-update) | async-done | bytes 5242896 | tf_op jit(solution)/shard_map/all_gather | solution.py:69
  137.5 9.2 %fusion.5 = f32[4,512,8,40]{1,3,2,0:T(8,128)} fusion(bf16[8,4,40,2048]{3,2,0,1:T(8,128)(2,1)} %all-gather.2.cloned.1.call-done, bf16[3,4,2048,512]{3,2,1,0:T(8,128)(2,1)} %add_convert_fusion), kind=kOutput, calls=%fused_computation.12 | convolution fusion | flops 2684354560 | bytes 16252928 | tf_op jit(solution)/shard_map/njqd,jdh->njqh/dot_general | solution.py:73
  146.7 8.8 %fusion.14 = bf16[8,4,40,512]{3,2,0,1:T(8,128)(2,1)S(1)} fusion(f32[4,512,8,40]{1,3,2,0:T(8,128)} %fusion.5, bf16[8,4,40,2048]{3,2,0,1:T(8,128)(2,1)} %all-gather.2.cloned.1.call-done, bf16[3,4,2048,512]{3,2,1,0:T(8,128)(2,1)} %add_convert_fusion), kind=kOutput, calls=%fused_computation.20 | convolution fusion | flops 2688286720 | bytes 17563648 | tf_op jit(solution)/shard_map/njqd,jdh->njqh/dot_general | solution.py:70
  155.5 3.3 gather_fusion
  158.7 20.4 %fusion.9 = f32[16,2,4,40,512]{4,3,1,2,0:T(8,128)} fusion(bf16[16,2,4,40,512]{4,3,1,2,0:T(8,128)(2,1)} %gather_fusion, pred[16]{0:T(512)(128)(4,1)S(1)} %get-tuple-element.25, bf16[16,4,256,512]{3,2,1,0:T(8,128)(2,1)} %gather_fusion.2, bf16[16,4,256,512]{3,2,1,0:T(8,128)(2,1)} %gather_fusion.1, pred[16]{0:T(512)(128)(4,1)S(1)} %get-tuple-element.26), kind=kOutput, calls=%fused_computation.17 | convolution fusion | flops 2770862080 | bytes 49283104 | tf_op jit(solution)/shard_map/cnjqh,cjfh->cnjqf/dot_general | solution.py:85
  179.2 0.9 copy-done.1
  180.1 6.9 %psum.14 = f32[128,8]{0,1:T(8,128)S(1)} all-reduce(f32[128,8]{0,1:T(8,128)S(1)} %fusion.36), channel_id=1, replica_groups=mesh['dp'=4,'expert'=2,'mp'=4] {'mp'}, use_global_device_ids=true, to_apply=%region_0.0 | all-reduce | flops 1024 | bytes 8192 | tf_op jit(solution)/shard_map/psum | solution.py:50
  187.1 110.1 %reduce-scatter.2.cloned.1.call-done = f32[1,2,4,40,512]{4,3,1,2,0:T(8,128)} async-done(((f32[16,2,4,40,512]{4,3,1,2,0:T(8,128)}), f32[1,2,4,40,512]{4,3,1,2,0:T(8,128)}) %reduce-scatter.2.cloned.1.call-update) | async-done | bytes 655376 | tf_op jit(solution)/shard_map/reduce_scatter | solution.py:84
  297.1 1.1 convert_bitcast_fusion
  299.0 3.5 all-to-all-start.1
  302.5 5.8 %all-to-all-done.1 = bf16[2,4,40,512]{3,2,1,0:T(8,128)(2,1)S(1)} async-done(((bf16[2,4,40,512]{3,2,1,0:T(8,128)(2,1)}), bf16[2,4,40,512]{3,2,1,0:T(8,128)(2,1)S(1)}, u32[]{:S(2)}, u32[]{:S(2)}) %all-to-all-start.1) | async-done | bytes 327712 | tf_op jit(solution)/shard_map/all_to_all | solution.py:93
  308.3 0.8 gather_fusion.4
  309.1 0.8 gather_fusion.3
  310.0 1.4 fusion.22
  311.4 39.5 %psum.15 = f32[]{:T(128)} all-reduce(f32[]{:T(128)} %get-tuple-element.11), channel_id=1, replica_groups=mesh['dp'=4,'expert'=2,'mp'=4] {'dp','expert','mp'}, use_global_device_ids=true, to_apply=%region_8.10 | all-reduce | flops 1 | bytes 8 | tf_op jit(solution)/shard_map/psum | solution.py:104
  (37 shorter events, 4.0 us)
Async XLA Ops:
  7.2 172.0 %copy-start = (bf16[512,8]{0,1:T(8,128)(2,1)S(1)}, bf16[512,8]{0,1:T(8,128)(2,1)}, u32[]{:S(2)}) copy-start(bf16[512,8]{0,1:T(8,128)(2,1)} %param.16) | copy-start | bytes 24580
  7.2 32.3 %copy-start.4 = (f32[2]{0:T(128)S(1)}, f32[2]{0:T(128)}, u32[]{:S(2)}) copy-start(f32[2]{0:T(128)} %param.21) | copy-start | bytes 28
  7.2 32.9 %copy-start.3 = (f32[2,4,512]{2,1,0:T(4,128)S(1)}, f32[2,4,512]{2,1,0:T(4,128)}, u32[]{:S(2)}) copy-start(f32[2,4,512]{2,1,0:T(4,128)} %param.20) | copy-start | bytes 49156
  7.2 130.3 %all-gather.2.cloned.1.call-start = ((), (), s32[]{:S(2)}) async-start(), calls=%async_computation.3 | async-start | bytes 6553600 | tf_op jit(solution)/shard_map/all_gather | solution.py:69
  39.4 257.7 %reduce-scatter.2.cloned.1.call-start = ((), (), s32[]{:S(2)}) async-start(), calls=%async_computation.4 | async-start | bytes 11141120 | tf_op jit(solution)/shard_map/reduce_scatter | solution.py:84
  179.1 0.9 copy-start.1
  179.1 130.8 %copy-start.2 = (bf16[128,512]{1,0:T(8,128)(2,1)S(1)}, bf16[128,512]{1,0:T(8,128)(2,1)}, u32[]{:S(2)}) copy-start(bf16[128,512]{1,0:T(8,128)(2,1)} %param.13) | copy-start | bytes 393220
  179.1 130.9 %copy-start.5 = (f32[128]{0:T(128)S(1)}, f32[128]{0:T(128)}, u32[]{:S(2)}) copy-start(f32[128]{0:T(128)} %param.14) | copy-start | bytes 1540
  299.0 9.3 %all-to-all-start.1 = ((bf16[2,4,40,512]{3,2,1,0:T(8,128)(2,1)}), bf16[2,4,40,512]{3,2,1,0:T(8,128)(2,1)S(1)}, u32[]{:S(2)}, u32[]{:S(2)}) async-start(bf16[2,4,40,512]{3,2,1,0:T(8,128)(2,1)} %copy.15), calls=%async_computation.2 | async-start | bytes 655360 | tf_op jit(solution)/shard_map/all_to_all | solution.py:93
Sparse Core Ops, SparseCore 0:
  39.5 97.9 all-gather.1
  179.3 117.8 reduce-scatter.1
where the time goes:
time: 360 us
  waiting for transfers between devices  146 us (41%)
  blocking collectives  74.9 us (21%)
  local copies, waits for them, and re-layouts  40.7 us (11%)
  other arithmetic  39.2 us (11%)
  matrix products  39.1 us (11%)
  between operations  16 us (4%)
    reduce_scatter x1, waiting for transfers between devices, per_device(): lax.psum_scatter(jnp.einsum('cnjqh,cjfh->cnjqf', chosen_rows, chosen_cols...  110 us
    psum x1, blocking collectives, per_device(): loss_total = lax.psum(partial_loss, ('dp', 'expert', 'mp'))  39.5 us
    convert_element_type x1, other arithmetic, rebuild(): return merged.astype(jnp.bfloat16)  34.5 us
    all_gather x1, waiting for transfers between devices, per_device(): shard_piece = lax.all_gather(slots, 'dp', axis=0, tiled=True)  30.2 us
    gather x3, local copies, waits for them, and re-layouts, per_device(): chosen_cols = jnp.take(down_blocks, positions % mp_count, axis=0)  24.2 us
    dot_general x1, matrix products, per_device(): jnp.einsum('cnjqh,cjfh->cnjqf', chosen_rows, chosen_cols, preferred_eleme...  20.4 us
    all_to_all x1, blocking collectives, per_device(): lax.all_to_all(buffer, 'expert', split_axis=0, concat_axis=0, tiled=True)  19.7 us
    dot_general x1, matrix products, per_device(): jnp.einsum('njqd,jdh->njqh', shard_piece, rebuilt[1], preferred_element_t...  9.21 us
  transfers between devices with their start and end apart: 3, of which 3 were waited for; matrix products, arithmetic and copies ran while one was open for 19% of the time, Pallas kernels for 0%

commit v1 on v0

--- a/solution.py
+++ b/solution.py
@@ -46,8 +46,15 @@
     expert_devices = lax.axis_size("expert")
     dp_count = lax.axis_size("dp")
     mp_count = lax.axis_size("mp")
-    partial_logits = jnp.dot(tokens, router_weight, preferred_element_type=jnp.float32)
-    logits = lax.psum(partial_logits, "mp")
+    stacked = jnp.concatenate([tokens, router_weight.T], axis=0)
+    gathered = lax.all_gather(stacked, "mp", axis=1, tiled=True)
+    source = gathered[:tok_rows]
+    logits = lax.dot_general(
+        source,
+        gathered[tok_rows:],
+        (((1,), (1,)), ((), ())),
+        preferred_element_type=jnp.float32,
+    )
     expert_ids = jnp.arange(expert_count, dtype=jnp.int32)
     pick_first = jnp.sum(jnp.where(routes[:, 0:1] == expert_ids[None, :], logits, 0.0), axis=1)
     pick_second = jnp.sum(jnp.where(routes[:, 1:2] == expert_ids[None, :], logits, 0.0), axis=1)
@@ -57,7 +64,6 @@
     placer = (
         flat_index[:, None] == jnp.arange(expert_count * CAP, dtype=jnp.int32)[None, :]
     ).astype(jnp.bfloat16)
-    source = lax.all_gather(tokens, "mp", axis=1, tiled=True)
     doubled = jnp.concatenate([source, source], axis=0)
     buffer = jnp.einsum("pk,pf->kf", placer, doubled, preferred_element_type=jnp.float32).astype(
         jnp.bfloat16
@@ -78,17 +84,11 @@
     down_blocks = (
         rebuilt[2].reshape(local_experts, mp_count, feat_local, hidden_local).transpose(1, 0, 2, 3)
     )
-    positions = jnp.arange(1 * lax.axis_size(("dp", "mp")), dtype=jnp.int32)
-    chosen_rows = jnp.take(hidden_groups, positions // mp_count, axis=0)
-    chosen_cols = jnp.take(down_blocks, positions % mp_count, axis=0)
-    summed = lax.psum_scatter(
-        jnp.einsum(
-            "cnjqh,cjfh->cnjqf", chosen_rows, chosen_cols, preferred_element_type=jnp.float32
-        ),
-        ("dp", "mp"),
-        scatter_dimension=0,
-        tiled=True,
+    partial = jnp.einsum(
+        "gnjqh,mjfh->gmnjqf", hidden_groups, down_blocks, preferred_element_type=jnp.float32
     )
+    partial = partial.reshape((dp_count * mp_count,) + partial.shape[2:])
+    summed = lax.psum_scatter(partial, ("dp", "mp"), scatter_dimension=0, tiled=True)
     expert_out = summed[0].astype(jnp.bfloat16)
     returned = lax.all_to_all(expert_out, "expert", split_axis=0, concat_axis=0, tiled=True)
     out_rows = returned.reshape(expert_count * CAP, feat_local)

time: 360 us -> 350 us (0.972)
  waiting for transfers between devices: 146 us -> 178 us
  local copies, waits for them, and re-layouts: 40.7 us -> 17 us
  matrix products: 39.1 us -> 25.9 us
  blocking collectives: 74.9 us -> 68 us
    gather x4 -> x0, local copies, waits for them, and re-layouts: 27.4 us -> none  [the longest x3 24.2 us: per_device(): chosen_cols = jnp.take(down_blocks, positions % mp_count, axis=0)]
    all_gather x1, waiting for transfers between devices: 30.2 us -> 54.4 us  [per_device(): shard_piece = lax.all_gather(slots, 'dp', axis=0, tiled=True)]
    dot_general x2, matrix products: 20.5 us -> 6.15 us  [the longest x1 5.9 us: per_device(): jnp.einsum('gnjqh,mjfh->gmnjqf', hidden_groups, down_blocks, preferred_el...]
    reduce_scatter x1, waiting for transfers between devices: 110 us -> 118 us  [per_device(): lax.psum_scatter(partial, ('dp', 'mp'), scatter_dimension=0, tiled=True)]
    psum x1 -> x0, blocking collectives: 6.89 us -> none  [per_device(): logits = lax.psum(partial_logits, 'mp')]
    transpose x0 -> x1, local copies, waits for them, and re-layouts: none -> 5.29 us  [per_device(): jnp.einsum('gnjqh,mjfh->gmnjqf', hidden_groups, down_blocks, preferred_el...]
  transfers between devices with their start and end apart: 3 -> 3, of which waited for: 3 -> 3; matrix products, arithmetic and copies ran while one was open for 19% -> 13% of each run, Pallas kernels for 0% -> 0%
where the time goes in v1:
time: 350 us; the launch traced here: 349 us
  waiting for transfers between devices  178 us (51%)
  blocking collectives  68 us (19%)
  other arithmetic  40.8 us (12%)
  matrix products  25.9 us (7%)
  local copies, waits for them, and re-layouts  17 us (5%)
  between operations  15.9 us (5%)
  starting transfers between devices  3.53 us (1%)
    reduce_scatter x1, waiting for transfers between devices, per_device(): lax.psum_scatter(partial, ('dp', 'mp'), scatter_dimension=0, tiled=True)  118 us
    all_gather x1, waiting for transfers between devices, per_device(): shard_piece = lax.all_gather(slots, 'dp', axis=0, tiled=True)  54.4 us
    psum x1, blocking collectives, per_device(): loss_total = lax.psum(partial_loss, ('dp', 'expert', 'mp'))  39.5 us
    convert_element_type x1, other arithmetic, rebuild(): return merged.astype(jnp.bfloat16)  34.5 us
    all_to_all x1, blocking collectives, per_device(): lax.all_to_all(buffer, 'expert', split_axis=0, concat_axis=0, tiled=True)  19.7 us
    dot_general x1, matrix products, per_device(): jnp.einsum('njqd,jdh->njqh', shard_piece, rebuilt[0], preferred_element_t...  9.89 us
    dot_general x1, matrix products, per_device(): jnp.einsum('njqd,jdh->njqh', shard_piece, rebuilt[1], preferred_element_t...  9.2 us
    all_gather x1, blocking collectives, per_device(): gathered = lax.all_gather(stacked, 'mp', axis=1, tiled=True)  8.83 us
  transfers between devices with their start and end apart: 3, of which 3 were waited for; matrix products, arithmetic and copies ran while one was open for 13% of the time, Pallas kernels for 0%

profile of v1, /device:TPU:0, one launch (start us, length us, event | category | flops | bytes accessed | tf_op | source)
XLA Modules:
  0.0 349.0 jit_solution(1344529401795927397)
XLA Ops:
  7.2 0.8 slice_bitcast_fusion.6
  8.0 0.6 reduce-window.6
  9.0 0.9 pad_maximum_fusion
  9.9 8.8 %all_gather.6 = bf16[136,2048]{1,0:T(8,128)(2,1)S(1)} all-gather(bf16[136,512]{1,0:T(8,128)(2,1)S(1)} %pad_maximum_fusion), channel_id=1, replica_groups=mesh['dp'=4,'expert'=2,'mp'=4] {'mp'}, dimensions={1}, use_global_device_ids=true | all-gather | bytes 696320 | tf_op jit(solution)/shard_map/all_gather | solution.py:50
  18.8 0.6 convolution_convert_fusion
  19.4 19.7 %all_to_all.10 = bf16[8,40,2048]{2,1,0:T(8,128)(2,1)S(1)} all-to-all(bf16[8,40,2048]{2,1,0:T(8,128)(2,1)S(1)} %bitcast.83), channel_id=1, replica_groups=mesh['dp'=4,'expert'=2,'mp'=4] {'expert'}, dimensions={0} | all-to-all | bytes 2621440 | tf_op jit(solution)/shard_map/all_to_all | solution.py:72
  39.1 1.2 copy.12
  40.3 0.6 fusion.20
  40.9 1.3 multiply_bitcast_fusion.1
  42.2 34.5 %add_convert_fusion = bf16[3,4,2048,512]{3,2,1,0:T(8,128)(2,1)} fusion(bf16[3,4,2048,512]{3,2,1,0:T(8,128)(2,1)} %param.19, bf16[3,4,2048,512]{3,2,1,0:T(8,128)(2,1)} %param.18, bf16[3,4,2048,512]{3,2,1,0:T(8,128)(2,1)} %param.17, f32[4,512]{1,0:T(4,128)S(1)} %get-tuple-element.12, f32[4,512]{1,0:T(4,128)S(1)} %get-tuple-element.11), kind=kLoop, calls=%fused_computation.2 | loop fusion | flops 100663296 | bytes 100679680 | tf_op jit(solution)/shard_map/convert_element_type | solution.py:17
  76.8 7.2 %slice.69 = bf16[1,4,2048,512]{3,2,1,0:T(8,128)(2,1)} slice(bf16[3,4,2048,512]{3,2,1,0:T(8,128)(2,1)} %add_convert_fusion), slice={[2:3], [0:4], [0:2048], [0:512]} | slice | bytes 16777216 | tf_op jit(solution)/shard_map/slice | solution.py:85
  83.9 54.4 %all-gather.2.cloned.1.call-done = bf16[8,4,40,2048]{3,2,0,1:T(8,128)(2,1)} async-done(((bf16[2,4,40,2048]{3,2,0,1:T(8,128)(2,1)}), bf16[8,4,40,2048]{3,2,0,1:T(8,128)(2,1)}) %all-gather.2.cloned.1.call-update) | async-done | bytes 5242896 | tf_op jit(solution)/shard_map/all_gather | solution.py:75
  138.3 9.2 %fusion = f32[4,512,8,40]{1,3,2,0:T(8,128)} fusion(bf16[8,4,40,2048]{3,2,0,1:T(8,128)(2,1)} %all-gather.2.cloned.1.call-done, bf16[3,4,2048,512]{3,2,1,0:T(8,128)(2,1)} %add_convert_fusion), kind=kOutput, calls=%fused_computation.4 | convolution fusion | flops 2684354560 | bytes 16252928 | tf_op jit(solution)/shard_map/njqd,jdh->njqh/dot_general | solution.py:79
  147.6 9.9 %fusion.2 = bf16[8,4,40,512]{3,2,0,1:T(8,128)(2,1)} fusion(f32[4,512,8,40]{1,3,2,0:T(8,128)} %fusion, bf16[8,4,40,2048]{3,2,0,1:T(8,128)(2,1)} %all-gather.2.cloned.1.call-done, bf16[3,4,2048,512]{3,2,1,0:T(8,128)(2,1)} %add_convert_fusion), kind=kOutput, calls=%fused_computation.10 | convolution fusion | flops 2688286720 | bytes 17563648 | tf_op jit(solution)/shard_map/njqd,jdh->njqh/dot_general | solution.py:76
  157.4 5.9 %convolution_bitcast_fusion = f32[4,4,2,4,40,512]{5,4,2,0,1,3:T(8,128)S(1)} fusion(bf16[4,4,512,512,1,1]{3,2,5,4,0,1:T(8,128)(2,1)} %bitcast.78, bf16[4,2,4,40,512,1]{4,3,1,0,5,2:T(8,128)(2,1)} %bitcast.82), kind=kOutput, calls=%fused_computation.7 | convolution fusion | flops 2684354560 | bytes 20185088 | tf_op jit(solution)/shard_map/gnjqh,mjfh->gmnjqf/dot_general | solution.py:87
  163.3 5.3 %copy.13 = f32[4,4,2,4,40,512]{5,4,3,2,1,0:T(8,128)} copy(f32[4,4,2,4,40,512]{5,4,2,0,1,3:T(8,128)S(1)} %convolution_bitcast_fusion) | data formatting | bytes 20971520 | tf_op jit(solution)/shard_map/gnjqh,mjfh->gmnjqf/transpose | solution.py:87
  169.0 117.7 %reduce-scatter.2.cloned.1.call-done = f32[1,2,4,40,512]{4,3,2,1,0:T(8,128)} async-done(((f32[16,2,4,40,512]{4,3,2,1,0:T(8,128)}), f32[1,2,4,40,512]{4,3,2,1,0:T(8,128)}) %reduce-scatter.2.cloned.1.call-update) | async-done | bytes 655376 | tf_op jit(solution)/shard_map/reduce_scatter | solution.py:91
  286.6 1.8 convert_bitcast_fusion
  288.5 3.5 all-to-all-start.1
  292.0 5.8 %all-to-all-done.1 = bf16[2,4,40,512]{3,2,1,0:T(8,128)(2,1)S(1)} async-done(((bf16[2,4,40,512]{3,2,1,0:T(8,128)(2,1)}), bf16[2,4,40,512]{3,2,1,0:T(8,128)(2,1)S(1)}, u32[]{:S(2)}, u32[]{:S(2)}) %all-to-all-start.1) | async-done | bytes 327712 | tf_op jit(solution)/shard_map/all_to_all | solution.py:93
  297.7 0.8 gather_fusion.1
  298.6 0.8 gather_fusion
  299.4 1.4 fusion.9
  300.9 39.5 %psum.7 = f32[]{:T(128)} all-reduce(f32[]{:T(128)} %get-tuple-element.9), channel_id=1, replica_groups=mesh['dp'=4,'expert'=2,'mp'=4] {'dp','expert','mp'}, use_global_device_ids=true, to_apply=%region_7.9 | all-reduce | flops 1 | bytes 8 | tf_op jit(solution)/shard_map/psum | solution.py:104
  (26 shorter events, 0.8 us)
Async XLA Ops:
  7.2 33.2 %copy-start.3 = (f32[2]{0:T(128)S(1)}, f32[2]{0:T(128)}, u32[]{:S(2)}) copy-start(f32[2]{0:T(128)} %param.21) | copy-start | bytes 28
  7.2 33.7 %copy-start.2 = (f32[2,4,512]{2,1,0:T(4,128)S(1)}, f32[2,4,512]{2,1,0:T(4,128)}, u32[]{:S(2)}) copy-start(f32[2,4,512]{2,1,0:T(4,128)} %param.20) | copy-start | bytes 49156
  7.2 131.2 %all-gather.2.cloned.1.call-start = ((), (), s32[]{:S(2)}) async-start(), calls=%async_computation.3 | async-start | bytes 6553600 | tf_op jit(solution)/shard_map/all_gather | solution.py:75
  40.3 246.4 %reduce-scatter.2.cloned.1.call-start = ((), (), s32[]{:S(2)}) async-start(), calls=%async_computation.4 | async-start | bytes 11141120 | tf_op jit(solution)/shard_map/reduce_scatter | solution.py:91
  168.6 130.8 %copy-start = (bf16[128,512]{1,0:T(8,128)(2,1)S(1)}, bf16[128,512]{1,0:T(8,128)(2,1)}, u32[]{:S(2)}) copy-start(bf16[128,512]{1,0:T(8,128)(2,1)} %param.12) | copy-start | bytes 393220
  168.6 130.8 %copy-start.1 = (bf16[128,512]{1,0:T(8,128)(2,1)S(1)}, bf16[128,512]{1,0:T(8,128)(2,1)}, u32[]{:S(2)}) copy-start(bf16[128,512]{1,0:T(8,128)(2,1)} %param.13) | copy-start | bytes 393220
  168.6 130.8 %copy-start.4 = (f32[128]{0:T(128)S(1)}, f32[128]{0:T(128)}, u32[]{:S(2)}) copy-start(f32[128]{0:T(128)} %param.14) | copy-start | bytes 1540
  288.5 9.2 %all-to-all-start.1 = ((bf16[2,4,40,512]{3,2,1,0:T(8,128)(2,1)}), bf16[2,4,40,512]{3,2,1,0:T(8,128)(2,1)S(1)}, u32[]{:S(2)}, u32[]{:S(2)}) async-start(bf16[2,4,40,512]{3,2,1,0:T(8,128)(2,1)} %convert_bitcast_fusion), calls=%async_computation.2 | async-start | bytes 655360 | tf_op jit(solution)/shard_map/all_to_all | solution.py:93
Sparse Core Ops, SparseCore 0:
  40.4 97.9 all-gather.1
  168.8 117.7 reduce-scatter.1
